TPU v7x, 32 devices: a whole 2x2x4 slice. The times are simulated.
32 devices in a mesh: dp: 8 (over z, y), mp: 4 (over x, core).
Axes of the slice: x: 2, y: 2, z: 4, core: 2. Of those that a mesh axis runs over, the one named last changes fastest.
Arguments:
- hidden: bfloat16 [5632, 7168], P('dp', 'mp'), may hold values from -0.1875 to 0.1875
- router_weight: bfloat16 [7168, 256], P(('mp', 'dp')), may hold values from -3 to 3
- logits: float32 [5632, 256], P(('dp', 'mp')), may hold values from -12 to 240
- first_pot: float32 [256], replicated, may hold values from -1 to 1
- second_pot: float32 [256], replicated, may hold values from -1 to 1
- expert_index: int32 [5632], P(('dp', 'mp')), may hold values from 0 to 255
- loss_grad: float32 [5632], P(('dp', 'mp')), may hold values from -9 to 9
Outputs:
- weight_grad: float32 [7168, 256], P(('mp', 'dp'))
- hidden_grad: bfloat16 [5632, 7168], P('dp', 'mp')
All inputs are finite; a program needn't handle non-finite values.
Results may differ from a plain program's by a relative error of at most 0.005.
Values may be sent and summed in bfloat16 or wider, within the bound.
A program may use at most 64 MiB of HBM per device.

v0:
```python
import jax
import jax.numpy as jnp
from jax import lax
from jax.sharding import PartitionSpec as P


def neg_lse(values):
    top = jnp.max(values, axis=1, keepdims=True)
    return -(top[:, 0] + jnp.log(jnp.sum(jnp.exp(values - top), axis=1)))


def body(hidden, router_weight, logits, first_pot, second_pot, expert_index, loss_grad):
    experts = logits.shape[1]
    total_tokens = logits.shape[0] * lax.axis_size("dp") * lax.axis_size("mp")
    ratio = experts / total_tokens
    first_row = neg_lse(logits)
    first_soft = jnp.exp(logits + first_row[:, None])
    shifted = logits + first_pot[None, :]
    second_row = neg_lse(shifted)
    second_soft = jnp.exp(shifted + second_row[:, None])
    first_col = ratio * jnp.exp(logits + first_row[:, None] + first_pot[None, :])
    prob = jnp.exp(logits + second_row[:, None] + second_pot[None, :])
    second_col = ratio * prob
    onehot = (expert_index[:, None] == jnp.arange(experts, dtype=jnp.int32)[None, :]).astype(
        jnp.float32
    )
    direct = onehot * prob * loss_grad[:, None]
    row_direct = jnp.sum(direct, axis=1)
    second_colgrad = lax.psum(jnp.sum(direct, axis=0), ("dp", "mp"))
    second_rowgrad = row_direct - jnp.dot(
        second_col, second_colgrad, precision=lax.Precision.HIGHEST
    )
    first_colgrad = lax.psum(-jnp.sum(second_rowgrad[:, None] * second_soft, axis=0), ("dp", "mp"))
    first_rowgrad = -jnp.dot(first_col, first_colgrad, precision=lax.Precision.HIGHEST)
    score_grad = (
        direct
        - second_colgrad[None, :] * second_col
        - second_rowgrad[:, None] * second_soft
        - first_colgrad[None, :] * first_col
        - first_rowgrad[:, None] * first_soft
    ).astype(jnp.bfloat16)
    score_full = lax.all_gather(score_grad, "mp", axis=0, tiled=True)
    hidden_grad = lax.dot_general(
        score_full,
        lax.all_gather(router_weight, "dp", axis=0, tiled=True),
        (((1,), (1,)), ((), ())),
        preferred_element_type=jnp.float32,
    ).astype(jnp.bfloat16)
    weight_grad = lax.psum_scatter(
        lax.dot_general(
            hidden, score_full, (((0,), (0,)), ((), ())), preferred_element_type=jnp.float32
        ),
        "dp",
        scatter_dimension=0,
        tiled=True,
    )
    return (weight_grad, hidden_grad)


def solution(mesh):
    in_specs = (
        P("dp", "mp"),
        P(("mp", "dp"), None),
        P(("dp", "mp"), None),
        P(),
        P(),
        P(("dp", "mp")),
        P(("dp", "mp")),
    )
    out_specs = (P(("mp", "dp"), None), P("dp", "mp"))
    return jax.shard_map(body, mesh=mesh, in_specs=in_specs, out_specs=out_specs, check_vma=False)
```

profile of v0, /device:TPU:0, one launch (start us, length us, event | category | flops | bytes accessed | tf_op | source)
XLA Modules:
  0.0 188.7 jit_solution(2244073612009030590)
XLA Ops:
  7.2 0.0 copy-start
  7.2 0.0 reduce-scatter.4.cloned.1.call-start
  7.2 1.2 fusion.15
  8.4 1.2 exponential_reduce_fusion
  9.6 1.2 fusion.5
  10.8 42.0 %psum.14 = f32[256]{0:T(256)S(1)} all-reduce(f32[256]{0:T(256)S(1)} %get-tuple-element.6), channel_id=1, replica_groups=mesh['dp'=8,'mp'=4] {'dp','mp'}, use_global_device_ids=true, to_apply=%region_3.0 | all-reduce | flops 256 | bytes 2048 | tf_op jit(solution)/shard_map/psum | solution.py:29
  52.8 1.2 fusion.2
  54.1 0.1 sub.34
  54.1 1.1 fusion.7
  55.2 40.1 %psum.15 = f32[256]{0:T(256)S(1)} all-reduce(f32[256]{0:T(256)S(1)} %neg.22), channel_id=1, replica_groups=mesh['dp'=8,'mp'=4] {'dp','mp'}, use_global_device_ids=true, to_apply=%region_8.0 | all-reduce | flops 256 | bytes 2048 | tf_op jit(solution)/shard_map/psum | solution.py:33
  95.3 1.2 fusion
  96.6 1.2 subtract_convert_fusion
  97.8 7.1 %all_gather.6 = bf16[704,256]{1,0:T(8,128)(2,1)S(1)} all-gather(bf16[176,256]{1,0:T(8,128)(2,1)S(1)} %subtract_convert_fusion), channel_id=1, replica_groups=mesh['dp'=8,'mp'=4] {'mp'}, dimensions={0}, use_global_device_ids=true | all-gather | bytes 450560 | tf_op jit(solution)/shard_map/all_gather | solution.py:42
  104.9 0.0 copy-done
  104.9 2.1 %convolution_bitcast_fusion = f32[1792,256]{0,1:T(8,128)} fusion(bf16[704,256]{1,0:T(8,128)(2,1)S(1)} %all_gather.6, bf16[704,1792]{1,0:T(8,128)(2,1)S(1)} %copy-done), kind=kOutput, calls=%fused_computation.1 | convolution fusion | flops 645922816 | bytes 4718592 | tf_op jit(solution)/shard_map/dot_general | solution.py:50
  107.0 0.0 copy-start.1
  107.0 2.8 %copy.11 = f32[1792,256]{1,0:T(8,128)} copy(f32[1792,256]{0,1:T(8,128)} %convolution_bitcast_fusion) | data formatting | bytes 3670016
  109.8 0.0 reduce-scatter.4.cloned.1.call-update
  109.8 0.0 copy-done.1
  109.8 34.5 %all_gather.7 = bf16[1792,256]{1,0:T(8,128)(2,1)S(1)} all-gather(bf16[224,256]{1,0:T(8,128)(2,1)S(1)} %copy-done.1), channel_id=1, replica_groups=mesh['dp'=8,'mp'=4] {'dp'}, dimensions={0}, use_global_device_ids=true | all-gather | bytes 1032192 | tf_op jit(solution)/shard_map/all_gather | solution.py:45
  144.4 2.3 %convolution_convert_fusion = bf16[704,1792]{1,0:T(8,128)(2,1)} fusion(bf16[704,256]{1,0:T(8,128)(2,1)S(1)} %all_gather.6, bf16[1792,256]{1,0:T(8,128)(2,1)S(1)} %all_gather.7), kind=kOutput, calls=%fused_computation | convolution fusion | flops 647184384 | bytes 3801088 | tf_op jit(solution)/shard_map/dot_general | solution.py:43
  146.7 35.1 %reduce-scatter.4.cloned.1.call-done = f32[224,256]{1,0:T(8,128)} async-done(((f32[1792,256]{1,0:T(8,128)}), f32[224,256]{1,0:T(8,128)}) %reduce-scatter.4.cloned.1.call-update) | async-done | bytes 229392
  (6 shorter events, 0.0 us)
Async XLA Ops:
  7.2 97.7 %copy-start = (bf16[704,1792]{1,0:T(8,128)(2,1)S(1)}, bf16[704,1792]{1,0:T(8,128)(2,1)}, u32[]{:S(2)}) copy-start(bf16[704,1792]{1,0:T(8,128)(2,1)} %param.7) | copy-start | bytes 7569412
  7.2 174.7 %reduce-scatter.4.cloned.1.call-start = ((), (), s32[]{:S(2)}) async-start(), calls=%async_computation.1 | async-start | bytes 2064384
  107.0 2.8 %copy-start.1 = (bf16[224,256]{1,0:T(8,128)(2,1)S(1)}, bf16[224,256]{1,0:T(8,128)(2,1)}, u32[]{:S(2)}) copy-start(bf16[224,256]{1,0:T(8,128)(2,1)} %param.8) | copy-start | bytes 344068
Sparse Core Ops, SparseCore 0:
  110.0 71.8 reduce-scatter.3
where the time goes:
time: 189 us
  blocking collectives  124 us (66%)
  waiting for transfers between devices  35.1 us (19%)
  between operations  14.1 us (7%)
  matrix products  6.93 us (4%)
  other arithmetic  5.94 us (3%)
  local copies, waits for them, and re-layouts  2.81 us (1%)
    psum x1, blocking collectives, body(): second_colgrad = lax.psum(jnp.sum(direct, axis=0), ('dp', 'mp'))  42 us
    psum x1, blocking collectives, body(): lax.psum(-jnp.sum(second_rowgrad[:, None] * second_soft, axis=0), ('dp',...  40.1 us
    unnamed x2, waiting for transfers between devices  35.1 us
    all_gather x1, blocking collectives, body(): lax.all_gather(router_weight, 'dp', axis=0, tiled=True)  34.5 us
    all_gather x1, blocking collectives, body(): score_full = lax.all_gather(score_grad, 'mp', axis=0, tiled=True)  7.07 us
  transfers between devices with their start and end apart: 1, of which 1 were waited for; matrix products, arithmetic and copies ran while one was open for 1% of the time, Pallas kernels for 0%

commit v1 on v0

--- a/solution.py
+++ b/solution.py
@@ -26,7 +26,9 @@
     )
     direct = onehot * prob * loss_grad[:, None]
     row_direct = jnp.sum(direct, axis=1)
-    second_colgrad = lax.psum(jnp.sum(direct, axis=0), ("dp", "mp"))
+    second_colgrad = jnp.sum(direct, axis=0)
+    for h in ("mp", "dp"):
+        second_colgrad = lax.psum(second_colgrad, h)
     second_rowgrad = row_direct - jnp.dot(
         second_col, second_colgrad, precision=lax.Precision.HIGHEST
     )

time: 189 us -> 173 us (0.915)
  blocking collectives: 124 us -> 109 us
    psum x1 -> x2, blocking collectives: 42 us -> 30 us  [body(): second_colgrad = lax.psum(second_colgrad, h)]
    psum x1, blocking collectives: 40.1 us -> 36.8 us  [body(): lax.psum(-jnp.sum(second_rowgrad[:, None] * second_soft, axis=0), ('dp',...]
where the time goes in v1:
time: 173 us
  blocking collectives  109 us (63%)
  waiting for transfers between devices  33.9 us (20%)
  between operations  14.1 us (8%)
  matrix products  6.93 us (4%)
  other arithmetic  5.94 us (3%)
  local copies, waits for them, and re-layouts  2.81 us (2%)
    psum x1, blocking collectives, body(): lax.psum(-jnp.sum(second_rowgrad[:, None] * second_soft, axis=0), ('dp',...  36.8 us
    all_gather x1, blocking collectives, body(): lax.all_gather(router_weight, 'dp', axis=0, tiled=True)  35.3 us
    unnamed x2, waiting for transfers between devices  33.9 us
    psum x2, blocking collectives, body(): second_colgrad = lax.psum(second_colgrad, h)  30 us
    all_gather x1, blocking collectives, body(): score_full = lax.all_gather(score_grad, 'mp', axis=0, tiled=True)  7.07 us
  transfers between devices with their start and end apart: 1, of which 1 were waited for; matrix products, arithmetic and copies ran while one was open for 1% of the time, Pallas kernels for 0%

profile of v1, /device:TPU:0, one launch (start us, length us, event | category | flops | bytes accessed | tf_op | source)
XLA Modules:
  0.0 173.0 jit_solution(4859562874453502369)
XLA Ops:
  7.2 0.0 copy-start
  7.2 0.0 reduce-scatter.4.cloned.1.call-start
  7.2 1.2 fusion.15
  8.4 1.2 exponential_reduce_fusion
  9.6 1.2 fusion.5
  10.8 8.4 %psum.21 = f32[256]{0:T(256)S(1)} all-reduce(f32[256]{0:T(256)S(1)} %get-tuple-element.6), channel_id=1, replica_groups=mesh['dp'=8,'mp'=4] {'mp'}, use_global_device_ids=true, to_apply=%region_3.0 | all-reduce | flops 256 | bytes 2048 | tf_op jit(solution)/shard_map/psum | solution.py:31
  19.2 21.7 %psum.22 = f32[256]{0:T(256)S(1)} all-reduce(f32[256]{0:T(256)S(1)} %psum.21), channel_id=1, replica_groups=mesh['dp'=8,'mp'=4] {'dp'}, use_global_device_ids=true, to_apply=%region_4.0 | all-reduce | flops 256 | bytes 2048 | tf_op jit(solution)/shard_map/psum | solution.py:31
  40.9 1.2 fusion.2
  42.1 0.1 sub.34
  42.2 1.1 fusion.7
  43.2 36.8 %psum.23 = f32[256]{0:T(256)S(1)} all-reduce(f32[256]{0:T(256)S(1)} %neg.22), channel_id=1, replica_groups=mesh['dp'=8,'mp'=4] {'dp','mp'}, use_global_device_ids=true, to_apply=%region_9.0 | all-reduce | flops 256 | bytes 2048 | tf_op jit(solution)/shard_map/psum | solution.py:35
  80.1 1.2 fusion
  81.4 1.2 subtract_convert_fusion
  82.6 7.1 %all_gather.6 = bf16[704,256]{1,0:T(8,128)(2,1)S(1)} all-gather(bf16[176,256]{1,0:T(8,128)(2,1)S(1)} %subtract_convert_fusion), channel_id=1, replica_groups=mesh['dp'=8,'mp'=4] {'mp'}, dimensions={0}, use_global_device_ids=true | all-gather | bytes 450560 | tf_op jit(solution)/shard_map/all_gather | solution.py:44
  89.6 0.0 copy-done
  89.6 2.1 %convolution_bitcast_fusion = f32[1792,256]{0,1:T(8,128)} fusion(bf16[704,256]{1,0:T(8,128)(2,1)S(1)} %all_gather.6, bf16[704,1792]{1,0:T(8,128)(2,1)S(1)} %copy-done), kind=kOutput, calls=%fused_computation.1 | convolution fusion | flops 645922816 | bytes 4718592 | tf_op jit(solution)/shard_map/dot_general | solution.py:52
  91.8 0.0 copy-start.1
  91.8 2.8 %copy.11 = f32[1792,256]{1,0:T(8,128)} copy(f32[1792,256]{0,1:T(8,128)} %convolution_bitcast_fusion) | data formatting | bytes 3670016
  94.6 0.0 reduce-scatter.4.cloned.1.call-update
  94.6 0.0 copy-done.1
  94.6 35.3 %all_gather.7 = bf16[1792,256]{1,0:T(8,128)(2,1)S(1)} all-gather(bf16[224,256]{1,0:T(8,128)(2,1)S(1)} %copy-done.1), channel_id=1, replica_groups=mesh['dp'=8,'mp'=4] {'dp'}, dimensions={0}, use_global_device_ids=true | all-gather | bytes 1032192 | tf_op jit(solution)/shard_map/all_gather | solution.py:47
  129.9 2.3 %convolution_convert_fusion = bf16[704,1792]{1,0:T(8,128)(2,1)} fusion(bf16[704,256]{1,0:T(8,128)(2,1)S(1)} %all_gather.6, bf16[1792,256]{1,0:T(8,128)(2,1)S(1)} %all_gather.7), kind=kOutput, calls=%fused_computation | convolution fusion | flops 647184384 | bytes 3801088 | tf_op jit(solution)/shard_map/dot_general | solution.py:45
  132.2 33.9 %reduce-scatter.4.cloned.1.call-done = f32[224,256]{1,0:T(8,128)} async-done(((f32[1792,256]{1,0:T(8,128)}), f32[224,256]{1,0:T(8,128)}) %reduce-scatter.4.cloned.1.call-update) | async-done | bytes 229392
  (6 shorter events, 0.0 us)
Async XLA Ops:
  7.2 82.5 %copy-start = (bf16[704,1792]{1,0:T(8,128)(2,1)S(1)}, bf16[704,1792]{1,0:T(8,128)(2,1)}, u32[]{:S(2)}) copy-start(bf16[704,1792]{1,0:T(8,128)(2,1)} %param.7) | copy-start | bytes 7569412
  7.2 159.0 %reduce-scatter.4.cloned.1.call-start = ((), (), s32[]{:S(2)}) async-start(), calls=%async_computation.1 | async-start | bytes 2064384
  91.8 2.8 %copy-start.1 = (bf16[224,256]{1,0:T(8,128)(2,1)S(1)}, bf16[224,256]{1,0:T(8,128)(2,1)}, u32[]{:S(2)}) copy-start(bf16[224,256]{1,0:T(8,128)(2,1)} %param.8) | copy-start | bytes 344068
Sparse Core Ops, SparseCore 0:
  94.7 71.3 reduce-scatter.3
